TPU v7x, 32 devices: a whole 2x2x4 slice. The times are simulated.
32 devices in a mesh: groups: 2 (over x), col: 16 (over z, y, core).
Axes of the slice: x: 2, y: 2, z: 4, core: 2. Of those that a mesh axis runs over, the one named last changes fastest.
Arguments:
- left: bfloat16 [256, 64, 32], P('col', 'groups'), parts along dimension 1, may hold values from -18 to 18
- right: bfloat16 [256, 2560, 32], P('col', 'groups'), parts along dimension 1, may hold values from -18 to 18
- out_weight: bfloat16 [1024, 128], replicated, may hold values from -0.1875 to 0.1875
- out_bias: float32 [128], replicated, may hold values from -3 to 3
Outputs:
- pair_update: bfloat16 [64, 1280, 128], P('groups', 'col'), parts along dimension 0
There are 2 independent parts, one for each index of `groups`. A program takes and returns all parts, laid end to end along the dimension named above; an argument that names none is the same for every part. Nothing has to cross between parts.
All inputs are finite; a program needn't handle non-finite values.
Results may differ from a plain program's by a relative error of at most 0.004.
Values may be sent and summed in bfloat16 or wider, within the bound.
A program may use at most 64 MiB of HBM per device.

v0:
```python
import jax
import jax.numpy as jnp
from jax import lax
from jax.sharding import PartitionSpec as P


def tile_update(left_rows, right_cols, out_weight, out_bias):
    seqs, count, width = left_rows.shape
    columns = right_cols.shape[1]
    outer = (
        jnp.einsum("sic,sje->ijce", left_rows, right_cols, preferred_element_type=jnp.float32)
        / seqs
    )
    flat = outer.astype(jnp.bfloat16).reshape(count * columns, width * width)
    update = jnp.dot(flat, out_weight, preferred_element_type=jnp.float32) + out_bias
    return update.astype(jnp.bfloat16).reshape(count, columns, out_weight.shape[1])


def rows_update(left_rows, right_cols, out_weight, out_bias):
    seqs, count, width = left_rows.shape
    blocks = jnp.transpose(left_rows.reshape(seqs, count // 8, 8, width), (1, 0, 2, 3))
    results = lax.map(lambda block: tile_update(block, right_cols, out_weight, out_bias), blocks)
    return results.reshape(count, right_cols.shape[1], out_weight.shape[1])


def on_device(left, right, out_weight, out_bias):
    left_part, right_cols = (
        lax.all_to_all(left, "col", split_axis=1, concat_axis=0, tiled=True),
        lax.all_to_all(right, "col", split_axis=1, concat_axis=0, tiled=True),
    )
    return rows_update(
        lax.all_gather(left_part, "col", axis=1, tiled=True), right_cols, out_weight, out_bias
    )


def solution(mesh):
    in_specs = (P("col", "groups", None), P("col", "groups", None), P(), P())
    out_specs = P("groups", "col", None)
    return jax.shard_map(
        on_device, mesh=mesh, in_specs=in_specs, out_specs=out_specs, check_vma=False
    )
```

profile of v0, /device:TPU:9, one launch (start us, length us, event | category | flops | bytes accessed | tf_op | source)
XLA Modules:
  0.0 118.3 jit_solution(4670310625103489706)
XLA Ops:
  0.0 1.0 copy.21
  1.0 0.8 reshape.16
  1.7 6.6 %all-to-all-start = ((bf16[16,2,512]{2,1,0:T(2,128)(2,1)}), bf16[16,2,512]{2,1,0:T(2,128)(2,1)S(1)}, u32[]{:S(2)}, u32[]{:S(2)}) async-start(bf16[16,2,512]{2,1,0:T(2,128)(2,1)} %reshape.16), calls=%async_computation | async-start | bytes 65536 | tf_op jit(solution)/shard_map/all_to_all | solution.py:28
  8.3 6.9 %copy.16 = bf16[16,1280,32]{2,0,1:T(8,128)(2,1)} copy(bf16[16,1280,32]{1,2,0:T(8,128)(2,1)} %param.7) | data formatting | bytes 2621440 | tf_op args[1]
  15.2 8.3 %reshape.18 = bf16[16,2,20480]{2,1,0:T(2,128)(2,1)} reshape(bf16[1280,16,32]{2,1,0:T(8,128)(2,1)} %bitcast.49) | data formatting | bytes 2621440
  23.5 6.0 %all-to-all-start.1 = ((bf16[16,2,20480]{2,1,0:T(2,128)(2,1)}), bf16[16,2,20480]{2,1,0:T(2,128)(2,1)S(1)}, u32[]{:S(2)}, u32[]{:S(2)}) async-start(bf16[16,2,20480]{2,1,0:T(2,128)(2,1)} %reshape.18), calls=%async_computation.1 | async-start | bytes 2621440 | tf_op jit(solution)/shard_map/all_to_all | solution.py:29
  29.8 43.8 %all_gather.3 = bf16[256,32,32]{0,2,1:T(8,128)(2,1)} all-gather(bf16[256,2,32]{0,2,1:T(8,128)(2,1)S(1)} %copy.15), channel_id=1, replica_groups=mesh['groups'=2,'col'=16] {'col'}, dimensions={1}, use_global_device_ids=true | all-gather | bytes 557056 | tf_op jit(solution)/shard_map/all_gather | solution.py:32
  73.6 4.0 %reshape.19 = bf16[1280,16,32]{2,1,0:T(8,128)(2,1)} reshape(bf16[16,2,20480]{2,1,0:T(2,128)(2,1)S(1)} %all-to-all-done.1) | data formatting | bytes 2621440
  77.6 6.8 %copy.17 = bf16[16,16,80,32]{2,3,0,1:T(8,128)(2,1)S(1)} copy(bf16[16,16,80,32]{3,0,2,1:T(8,128)(2,1)} %bitcast.48) | data formatting | bytes 2621440 | tf_op jit(solution)/shard_map/all_to_all | solution.py:29
  84.4 1.6 %copy.18 = bf16[256,80,32]{0,1,2:T(8,128)(2,1)S(1)} copy(bf16[256,80,32]{1,2,0:T(8,128)(2,1)S(1)} %bitcast.51) | data formatting | bytes 2621440 | tf_op jit(solution)/shard_map/while | solution.py:22
  86.0 32.3 %while.10 = (s32[]{:T(128)}, bf16[4,8,80,128]{3,2,1,0:T(8,128)(2,1)}, bf16[4,256,8,32]{1,3,2,0:T(8,128)(2,1)}, bf16[256,80,32]{0,1,2:T(8,128)(2,1)S(1)}, bf16[10...) while((s32[]{:T(128)}, bf16[4,8,80,128]{3,2,1,0:T(8,128)(2,1)}, bf16[4,256,8,32]{1,3,2,0:T(8,128)(2,1)}, ...), condition=%wide.region_1.2_spmd, body=%wide.region_0.1_spmd.sunk | while | flops 504791040 | bytes 20547204 | solution.py:22
  86.0 1.1 copy-done
  87.1 1.6 %fusion.18 = bf16[8,80,32,32]{1,2,3,0:T(8,128)(2,1)S(1)} fusion(bf16[256,80,32]{0,1,2:T(8,128)(2,1)S(1)} %get-tuple-element.116, bf16[4,256,8,32]{1,3,2,0:T(8,128)(2,1)} %get-tuple-element.115, s32[]{:T(128)} %get-tuple-element.106), kind=kOutput, calls=%fused_computation.1.clone.1 | convolution fusion | flops 336855040 | bytes 2753024 | tf_op jit(solution)/shard_map/while/body/eval_jaxpr/sic,sje->ijce/dot_general | solution.py:11
  88.7 1.4 %copy.23 = bf16[8,80,32,32]{1,0,3,2:T(8,128)(2,1)S(1)} copy(bf16[8,80,32,32]{1,2,3,0:T(8,128)(2,1)S(1)} %fusion.18) | data formatting | bytes 2621440 | tf_op jit(solution)/shard_map/while/body/eval_jaxpr/convert_element_type | solution.py:14
  90.1 1.7 %reshape.21 = bf16[640,1024]{0,1:T(8,128)(2,1)S(1)} reshape(bf16[8,80,32,32]{1,0,3,2:T(8,128)(2,1)S(1)} %copy.23) | data formatting | bytes 2621440 | tf_op jit(solution)/shard_map/while/body/eval_jaxpr/reshape | solution.py:14
  91.8 1.6 %fusion.19 = bf16[640,128]{1,0:T(8,128)(2,1)S(1)} fusion(bf16[640,1024]{0,1:T(8,128)(2,1)S(1)} %reshape.21, bf16[1024,128]{1,0:T(8,128)(2,1)} %get-tuple-element.117, f32[128]{0:T(128)S(1)} %get-tuple-element.118), kind=kOutput, calls=%fused_computation.4.clone.1 | convolution fusion | flops 167936000 | bytes 1737216 | tf_op jit(solution)/shard_map/while/body/eval_jaxpr/dot_general | solution.py:15
  93.4 0.7 constant_dynamic-update-slice_fusion.2
  94.1 1.1 copy-done
  95.2 1.6 %fusion.18 = bf16[8,80,32,32]{1,2,3,0:T(8,128)(2,1)S(1)} fusion(bf16[256,80,32]{0,1,2:T(8,128)(2,1)S(1)} %get-tuple-element.116, bf16[4,256,8,32]{1,3,2,0:T(8,128)(2,1)} %get-tuple-element.115, s32[]{:T(128)} %get-tuple-element.106), kind=kOutput, calls=%fused_computation.1.clone.1 | convolution fusion | flops 336855040 | bytes 2753024 | tf_op jit(solution)/shard_map/while/body/eval_jaxpr/sic,sje->ijce/dot_general | solution.py:11
  96.8 1.4 %copy.23 = bf16[8,80,32,32]{1,0,3,2:T(8,128)(2,1)S(1)} copy(bf16[8,80,32,32]{1,2,3,0:T(8,128)(2,1)S(1)} %fusion.18) | data formatting | bytes 2621440 | tf_op jit(solution)/shard_map/while/body/eval_jaxpr/convert_element_type | solution.py:14
  98.2 1.7 %reshape.21 = bf16[640,1024]{0,1:T(8,128)(2,1)S(1)} reshape(bf16[8,80,32,32]{1,0,3,2:T(8,128)(2,1)S(1)} %copy.23) | data formatting | bytes 2621440 | tf_op jit(solution)/shard_map/while/body/eval_jaxpr/reshape | solution.py:14
  99.9 1.6 %fusion.19 = bf16[640,128]{1,0:T(8,128)(2,1)S(1)} fusion(bf16[640,1024]{0,1:T(8,128)(2,1)S(1)} %reshape.21, bf16[1024,128]{1,0:T(8,128)(2,1)} %get-tuple-element.117, f32[128]{0:T(128)S(1)} %get-tuple-element.118), kind=kOutput, calls=%fused_computation.4.clone.1 | convolution fusion | flops 167936000 | bytes 1737216 | tf_op jit(solution)/shard_map/while/body/eval_jaxpr/dot_general | solution.py:15
  102.2 1.1 copy-done
  103.2 1.6 %fusion.18 = bf16[8,80,32,32]{1,2,3,0:T(8,128)(2,1)S(1)} fusion(bf16[256,80,32]{0,1,2:T(8,128)(2,1)S(1)} %get-tuple-element.116, bf16[4,256,8,32]{1,3,2,0:T(8,128)(2,1)} %get-tuple-element.115, s32[]{:T(128)} %get-tuple-element.106), kind=kOutput, calls=%fused_computation.1.clone.1 | convolution fusion | flops 336855040 | bytes 2753024 | tf_op jit(solution)/shard_map/while/body/eval_jaxpr/sic,sje->ijce/dot_general | solution.py:11
  104.9 1.4 %copy.23 = bf16[8,80,32,32]{1,0,3,2:T(8,128)(2,1)S(1)} copy(bf16[8,80,32,32]{1,2,3,0:T(8,128)(2,1)S(1)} %fusion.18) | data formatting | bytes 2621440 | tf_op jit(solution)/shard_map/while/body/eval_jaxpr/convert_element_type | solution.py:14
  106.2 1.7 %reshape.21 = bf16[640,1024]{0,1:T(8,128)(2,1)S(1)} reshape(bf16[8,80,32,32]{1,0,3,2:T(8,128)(2,1)S(1)} %copy.23) | data formatting | bytes 2621440 | tf_op jit(solution)/shard_map/while/body/eval_jaxpr/reshape | solution.py:14
  108.0 1.6 %fusion.19 = bf16[640,128]{1,0:T(8,128)(2,1)S(1)} fusion(bf16[640,1024]{0,1:T(8,128)(2,1)S(1)} %reshape.21, bf16[1024,128]{1,0:T(8,128)(2,1)} %get-tuple-element.117, f32[128]{0:T(128)S(1)} %get-tuple-element.118), kind=kOutput, calls=%fused_computation.4.clone.1 | convolution fusion | flops 167936000 | bytes 1737216 | tf_op jit(solution)/shard_map/while/body/eval_jaxpr/dot_general | solution.py:15
  110.2 1.1 copy-done
  111.3 1.6 %fusion.18 = bf16[8,80,32,32]{1,2,3,0:T(8,128)(2,1)S(1)} fusion(bf16[256,80,32]{0,1,2:T(8,128)(2,1)S(1)} %get-tuple-element.116, bf16[4,256,8,32]{1,3,2,0:T(8,128)(2,1)} %get-tuple-element.115, s32[]{:T(128)} %get-tuple-element.106), kind=kOutput, calls=%fused_computation.1.clone.1 | convolution fusion | flops 336855040 | bytes 2753024 | tf_op jit(solution)/shard_map/while/body/eval_jaxpr/sic,sje->ijce/dot_general | solution.py:11
  113.0 1.4 %copy.23 = bf16[8,80,32,32]{1,0,3,2:T(8,128)(2,1)S(1)} copy(bf16[8,80,32,32]{1,2,3,0:T(8,128)(2,1)S(1)} %fusion.18) | data formatting | bytes 2621440 | tf_op jit(solution)/shard_map/while/body/eval_jaxpr/convert_element_type | solution.py:14
  114.3 1.7 %reshape.21 = bf16[640,1024]{0,1:T(8,128)(2,1)S(1)} reshape(bf16[8,80,32,32]{1,0,3,2:T(8,128)(2,1)S(1)} %copy.23) | data formatting | bytes 2621440 | tf_op jit(solution)/shard_map/while/body/eval_jaxpr/reshape | solution.py:14
  116.0 1.6 %fusion.19 = bf16[640,128]{1,0:T(8,128)(2,1)S(1)} fusion(bf16[640,1024]{0,1:T(8,128)(2,1)S(1)} %reshape.21, bf16[1024,128]{1,0:T(8,128)(2,1)} %get-tuple-element.117, f32[128]{0:T(128)S(1)} %get-tuple-element.118), kind=kOutput, calls=%fused_computation.4.clone.1 | convolution fusion | flops 167936000 | bytes 1737216 | tf_op jit(solution)/shard_map/while/body/eval_jaxpr/dot_general | solution.py:15
  (23 shorter events, 2.3 us)
Async XLA Ops:
  1.7 21.8 %all-to-all-start = ((bf16[16,2,512]{2,1,0:T(2,128)(2,1)}), bf16[16,2,512]{2,1,0:T(2,128)(2,1)S(1)}, u32[]{:S(2)}, u32[]{:S(2)}) async-start(bf16[16,2,512]{2,1,0:T(2,128)(2,1)} %reshape.16), calls=%async_computation | async-start | bytes 65536 | tf_op jit(solution)/shard_map/all_to_all | solution.py:28
  23.5 50.1 %all-to-all-start.1 = ((bf16[16,2,20480]{2,1,0:T(2,128)(2,1)}), bf16[16,2,20480]{2,1,0:T(2,128)(2,1)S(1)}, u32[]{:S(2)}, u32[]{:S(2)}) async-start(bf16[16,2,20480]{2,1,0:T(2,128)(2,1)} %reshape.18), calls=%async_computation.1 | async-start | bytes 2621440 | tf_op jit(solution)/shard_map/all_to_all | solution.py:29
  84.4 1.6 %copy-start.2 = (f32[128]{0:T(128)S(1)}, f32[128]{0:T(128)}, u32[]{:S(2)}) copy-start(f32[128]{0:T(128)} %param.9) | copy-start | bytes 1540
  86.0 1.1 copy-start
  91.8 2.3 %copy-start.1 = (bf16[256,80,32]{0,1,2:T(8,128)(2,1)S(1)}, bf16[256,80,32]{0,1,2:T(8,128)(2,1)}, u32[]{:S(2)}) copy-start(bf16[256,80,32]{0,1,2:T(8,128)(2,1)} %copy-done) | copy-start | bytes 3932164 | tf_op jit(solution)/shard_map/while
  94.1 1.1 copy-start
  99.9 2.3 %copy-start.1 = (bf16[256,80,32]{0,1,2:T(8,128)(2,1)S(1)}, bf16[256,80,32]{0,1,2:T(8,128)(2,1)}, u32[]{:S(2)}) copy-start(bf16[256,80,32]{0,1,2:T(8,128)(2,1)} %copy-done) | copy-start | bytes 3932164 | tf_op jit(solution)/shard_map/while
  102.2 1.1 copy-start
  107.9 2.3 %copy-start.1 = (bf16[256,80,32]{0,1,2:T(8,128)(2,1)S(1)}, bf16[256,80,32]{0,1,2:T(8,128)(2,1)}, u32[]{:S(2)}) copy-start(bf16[256,80,32]{0,1,2:T(8,128)(2,1)} %copy-done) | copy-start | bytes 3932164 | tf_op jit(solution)/shard_map/while
  110.2 1.1 copy-start
  116.0 2.3 %copy-start.1 = (bf16[256,80,32]{0,1,2:T(8,128)(2,1)S(1)}, bf16[256,80,32]{0,1,2:T(8,128)(2,1)}, u32[]{:S(2)}) copy-start(bf16[256,80,32]{0,1,2:T(8,128)(2,1)} %copy-done) | copy-start | bytes 3932164 | tf_op jit(solution)/shard_map/while
where the time goes:
time: 119 us; the launch traced here: 118 us
  local copies, waits for them, and re-layouts  48.7 us (41%)
  blocking collectives  43.8 us (37%)
  matrix products  12.9 us (11%)
  starting transfers between devices  12.6 us (11%)
    all_gather x1, blocking collectives, on_device(): lax.all_gather(left_part, 'col', axis=1, tiled=True)  43.8 us
    unnamed x8, local copies, waits for them, and re-layouts  21.1 us
    reshape x4, local copies, waits for them, and re-layouts, tile_update(): flat = outer.astype(jnp.bfloat16).reshape(count * columns, width * width)  6.79 us
    all_to_all x1, local copies, waits for them, and re-layouts, on_device(): lax.all_to_all(right, 'col', split_axis=1, concat_axis=0, tiled=True)  6.76 us
    all_to_all x1, starting transfers between devices, on_device(): lax.all_to_all(left, 'col', split_axis=1, concat_axis=0, tiled=True)  6.58 us
    dot_general x4, matrix products, tile_update(): jnp.einsum('sic,sje->ijce', left_rows, right_cols, preferred_element_type...  6.53 us
    dot_general x4, matrix products, tile_update(): jnp.dot(flat, out_weight, preferred_element_type=jnp.float32) + out_bias  6.39 us
    all_to_all x1, starting transfers between devices, on_device(): lax.all_to_all(right, 'col', split_axis=1, concat_axis=0, tiled=True)  6.02 us
  transfers between devices with their start and end apart: 2, of which 0 were waited for; matrix products, arithmetic and copies ran while one was open for 13% of the time, Pallas kernels for 0%

commit v1 on v0

--- a/solution.py
+++ b/solution.py
@@ -2,6 +2,18 @@
 import jax.numpy as jnp
 from jax import lax
 from jax.sharding import PartitionSpec as P
+
+
+def collect(array, axis, dim):
+    ways, here = (lax.axis_size(axis), lax.axis_index(axis))
+    grown, reach = (array, 1)
+    while reach < ways:
+        theirs = lax.ppermute(grown, axis, [(d, d ^ reach) for d in range(ways)])
+        mine_first = jnp.concatenate([grown, theirs], axis=dim)
+        theirs_first = jnp.concatenate([theirs, grown], axis=dim)
+        grown = jnp.where(here & reach == 0, mine_first, theirs_first)
+        reach = 2 * reach
+    return grown
 
 
 def tile_update(left_rows, right_cols, out_weight, out_bias):
@@ -28,9 +40,7 @@
         lax.all_to_all(left, "col", split_axis=1, concat_axis=0, tiled=True),
         lax.all_to_all(right, "col", split_axis=1, concat_axis=0, tiled=True),
     )
-    return rows_update(
-        lax.all_gather(left_part, "col", axis=1, tiled=True), right_cols, out_weight, out_bias
-    )
+    return rows_update(collect(left_part, "col", 1), right_cols, out_weight, out_bias)
 
 
 def solution(mesh):

time: 119 us -> 120 us (level)
  the two profiles are of different devices: /device:TPU:9 before, /device:TPU:0 now
where the time goes in v1:
time: 120 us; the launch traced here: 119 us
  local copies, waits for them, and re-layouts  48.9 us (41%)
  waiting for transfers between devices  36.1 us (30%)
  starting transfers between devices  20.3 us (17%)
  matrix products  12.9 us (11%)
    ppermute x4, waiting for transfers between devices, collect(): theirs = lax.ppermute(grown, axis, [(d, d ^ reach) for d in range(ways)])  36.1 us
    unnamed x8, local copies, waits for them, and re-layouts  21.1 us
    all_to_all x1, starting transfers between devices, on_device(): lax.all_to_all(left, 'col', split_axis=1, concat_axis=0, tiled=True)  7.41 us
    ppermute x4, starting transfers between devices, collect(): theirs = lax.ppermute(grown, axis, [(d, d ^ reach) for d in range(ways)])  6.92 us
    reshape x4, local copies, waits for them, and re-layouts, tile_update(): flat = outer.astype(jnp.bfloat16).reshape(count * columns, width * width)  6.79 us
    all_to_all x1, local copies, waits for them, and re-layouts, on_device(): lax.all_to_all(right, 'col', split_axis=1, concat_axis=0, tiled=True)  6.76 us
    dot_general x4, matrix products, tile_update(): jnp.einsum('sic,sje->ijce', left_rows, right_cols, preferred_element_type...  6.52 us
    dot_general x4, matrix products, tile_update(): jnp.dot(flat, out_weight, preferred_element_type=jnp.float32) + out_bias  6.39 us
  transfers between devices with their start and end apart: 6, of which 4 were waited for; matrix products, arithmetic and copies ran while one was open for 14% of the time, Pallas kernels for 0%

profile of v1, /device:TPU:0, one launch (start us, length us, event | category | flops | bytes accessed | tf_op | source)
XLA Modules:
  0.0 119.5 jit_solution(3331219254307533619)
XLA Ops:
  1.7 7.4 %all-to-all-start = ((bf16[16,2,512]{2,1,0:T(2,128)(2,1)}), bf16[16,2,512]{2,1,0:T(2,128)(2,1)S(1)}, u32[]{:S(2)}, u32[]{:S(2)}) async-start(bf16[16,2,512]{2,1,0:T(2,128)(2,1)} %reshape.17), calls=%async_computation | async-start | bytes 65536 | tf_op jit(solution)/shard_map/all_to_all | solution.py:40
  9.1 6.9 %copy.19 = bf16[16,1280,32]{2,0,1:T(8,128)(2,1)} copy(bf16[16,1280,32]{1,2,0:T(8,128)(2,1)} %param.7) | data formatting | bytes 2621440 | tf_op args[1]
  16.0 8.3 %reshape.19 = bf16[16,2,20480]{2,1,0:T(2,128)(2,1)} reshape(bf16[1280,16,32]{2,1,0:T(8,128)(2,1)} %bitcast.49) | data formatting | bytes 2621440
  24.4 6.0 %all-to-all-start.1 = ((bf16[16,2,20480]{2,1,0:T(2,128)(2,1)}), bf16[16,2,20480]{2,1,0:T(2,128)(2,1)S(1)}, u32[]{:S(2)}, u32[]{:S(2)}) async-start(bf16[16,2,20480]{2,1,0:T(2,128)(2,1)} %reshape.19), calls=%async_computation.1 | async-start | bytes 2621440 | tf_op jit(solution)/shard_map/all_to_all | solution.py:41
  32.1 1.9 %collective-permute-start.1 = (bf16[256,4,32]{0,2,1:T(8,128)(2,1)S(1)}, bf16[256,4,32]{0,2,1:T(8,128)(2,1)S(1)}, u32[]{:S(2)}, u32[]{:S(2)}) collective-permute-start(bf16[256,4,32]{0,2,1:T(8,128)(2,1)S(1)} %maximum_select_fusion.3), channel_id=1, source_target_pairs={{0,2},{1,3},{2,0},{3,1},{4,6},{5,7},{6,4},{7,5},{8,10},{9,11},{10,... | collective-permute-start | bytes 196616 | tf_op jit(solution)/shard_map/ppermute | solution.py:11
  34.0 8.8 %collective-permute-done.1 = bf16[256,4,32]{0,2,1:T(8,128)(2,1)S(1)} collective-permute-done((bf16[256,4,32]{0,2,1:T(8,128)(2,1)S(1)}, bf16[256,4,32]{0,2,1:T(8,128)(2,1)S(1)}, u32[]{:S(2)}, u32[]{:S(2)}) %collective-permute-start.1) | collective-permute-done | bytes 65568 | tf_op jit(solution)/shard_map/ppermute | solution.py:11
  42.9 12.6 %collective-permute-done.2 = bf16[256,8,32]{0,2,1:T(8,128)(2,1)S(1)} collective-permute-done((bf16[256,8,32]{0,2,1:T(8,128)(2,1)S(1)}, bf16[256,8,32]{0,2,1:T(8,128)(2,1)S(1)}, u32[]{:S(2)}, u32[]{:S(2)}) %collective-permute-start.2) | collective-permute-done | bytes 131104 | tf_op jit(solution)/shard_map/ppermute | solution.py:11
  55.5 4.4 %collective-permute-start.3 = (bf16[256,16,32]{0,2,1:T(8,128)(2,1)S(1)}, bf16[256,16,32]{0,2,1:T(8,128)(2,1)S(1)}, u32[]{:S(2)}, u32[]{:S(2)}) collective-permute-start(bf16[256,16,32]{0,2,1:T(8,128)(2,1)S(1)} %maximum_select_fusion.1), channel_id=1, source_target_pairs={{0,8},{1,9},{2,10},{3,11},{4,12},{5,13},{6,14},{7,15},{8,0},{9,1},... | collective-permute-start | bytes 786440 | tf_op jit(solution)/shard_map/ppermute | solution.py:11
  59.9 13.8 %collective-permute-done.3 = bf16[256,16,32]{0,2,1:T(8,128)(2,1)S(1)} collective-permute-done((bf16[256,16,32]{0,2,1:T(8,128)(2,1)S(1)}, bf16[256,16,32]{0,2,1:T(8,128)(2,1)S(1)}, u32[]{:S(2)}, u32[]{:S(2)}) %collective-permute-start.3) | collective-permute-done | bytes 262176 | tf_op jit(solution)/shard_map/ppermute | solution.py:11
  74.7 4.0 %reshape.20 = bf16[1280,16,32]{2,1,0:T(8,128)(2,1)} reshape(bf16[16,2,20480]{2,1,0:T(2,128)(2,1)S(1)} %all-to-all-done.1) | data formatting | bytes 2621440
  78.7 6.8 %copy.20 = bf16[16,16,80,32]{2,3,0,1:T(8,128)(2,1)S(1)} copy(bf16[16,16,80,32]{3,0,2,1:T(8,128)(2,1)} %bitcast.48) | data formatting | bytes 2621440 | tf_op jit(solution)/shard_map/all_to_all | solution.py:41
  85.5 1.6 %copy.21 = bf16[256,80,32]{0,1,2:T(8,128)(2,1)S(1)} copy(bf16[256,80,32]{1,2,0:T(8,128)(2,1)S(1)} %bitcast.51) | data formatting | bytes 2621440 | tf_op jit(solution)/shard_map/while | solution.py:34
  87.1 32.4 %while.10 = (s32[]{:T(128)}, bf16[4,8,80,128]{3,2,1,0:T(8,128)(2,1)}, bf16[4,256,8,32]{1,3,2,0:T(8,128)(2,1)}, bf16[256,80,32]{0,1,2:T(8,128)(2,1)S(1)}, bf16[10...) while((s32[]{:T(128)}, bf16[4,8,80,128]{3,2,1,0:T(8,128)(2,1)}, bf16[4,256,8,32]{1,3,2,0:T(8,128)(2,1)}, ...), condition=%wide.region_1.2_spmd, body=%wide.region_0.1_spmd.sunk | while | flops 504791040 | bytes 20547204 | solution.py:34
  88.2 1.6 %fusion.18 = bf16[8,80,32,32]{1,2,3,0:T(8,128)(2,1)S(1)} fusion(bf16[256,80,32]{0,1,2:T(8,128)(2,1)S(1)} %get-tuple-element.116, bf16[4,256,8,32]{1,3,2,0:T(8,128)(2,1)} %get-tuple-element.115, s32[]{:T(128)} %get-tuple-element.106), kind=kOutput, calls=%fused_computation.1.clone.1 | convolution fusion | flops 336855040 | bytes 2753024 | tf_op jit(solution)/shard_map/while/body/eval_jaxpr/sic,sje->ijce/dot_general | solution.py:23
  89.8 1.4 %copy.26 = bf16[8,80,32,32]{1,0,3,2:T(8,128)(2,1)S(1)} copy(bf16[8,80,32,32]{1,2,3,0:T(8,128)(2,1)S(1)} %fusion.18) | data formatting | bytes 2621440 | tf_op jit(solution)/shard_map/while/body/eval_jaxpr/convert_element_type | solution.py:26
  91.2 1.7 %reshape.22 = bf16[640,1024]{0,1:T(8,128)(2,1)S(1)} reshape(bf16[8,80,32,32]{1,0,3,2:T(8,128)(2,1)S(1)} %copy.26) | data formatting | bytes 2621440 | tf_op jit(solution)/shard_map/while/body/eval_jaxpr/reshape | solution.py:26
  92.9 1.6 %fusion.19 = bf16[640,128]{1,0:T(8,128)(2,1)S(1)} fusion(bf16[640,1024]{0,1:T(8,128)(2,1)S(1)} %reshape.22, bf16[1024,128]{1,0:T(8,128)(2,1)} %get-tuple-element.117, f32[128]{0:T(128)S(1)} %get-tuple-element.118), kind=kOutput, calls=%fused_computation.4.clone.1 | convolution fusion | flops 167936000 | bytes 1737216 | tf_op jit(solution)/shard_map/while/body/eval_jaxpr/dot_general | solution.py:27
  95.2 1.1 copy-done
  96.3 1.6 %fusion.18 = bf16[8,80,32,32]{1,2,3,0:T(8,128)(2,1)S(1)} fusion(bf16[256,80,32]{0,1,2:T(8,128)(2,1)S(1)} %get-tuple-element.116, bf16[4,256,8,32]{1,3,2,0:T(8,128)(2,1)} %get-tuple-element.115, s32[]{:T(128)} %get-tuple-element.106), kind=kOutput, calls=%fused_computation.1.clone.1 | convolution fusion | flops 336855040 | bytes 2753024 | tf_op jit(solution)/shard_map/while/body/eval_jaxpr/sic,sje->ijce/dot_general | solution.py:23
  97.9 1.4 %copy.26 = bf16[8,80,32,32]{1,0,3,2:T(8,128)(2,1)S(1)} copy(bf16[8,80,32,32]{1,2,3,0:T(8,128)(2,1)S(1)} %fusion.18) | data formatting | bytes 2621440 | tf_op jit(solution)/shard_map/while/body/eval_jaxpr/convert_element_type | solution.py:26
  99.3 1.7 %reshape.22 = bf16[640,1024]{0,1:T(8,128)(2,1)S(1)} reshape(bf16[8,80,32,32]{1,0,3,2:T(8,128)(2,1)S(1)} %copy.26) | data formatting | bytes 2621440 | tf_op jit(solution)/shard_map/while/body/eval_jaxpr/reshape | solution.py:26
  101.0 1.6 %fusion.19 = bf16[640,128]{1,0:T(8,128)(2,1)S(1)} fusion(bf16[640,1024]{0,1:T(8,128)(2,1)S(1)} %reshape.22, bf16[1024,128]{1,0:T(8,128)(2,1)} %get-tuple-element.117, f32[128]{0:T(128)S(1)} %get-tuple-element.118), kind=kOutput, calls=%fused_computation.4.clone.1 | convolution fusion | flops 167936000 | bytes 1737216 | tf_op jit(solution)/shard_map/while/body/eval_jaxpr/dot_general | solution.py:27
  103.3 1.1 copy-done
  104.4 1.6 %fusion.18 = bf16[8,80,32,32]{1,2,3,0:T(8,128)(2,1)S(1)} fusion(bf16[256,80,32]{0,1,2:T(8,128)(2,1)S(1)} %get-tuple-element.116, bf16[4,256,8,32]{1,3,2,0:T(8,128)(2,1)} %get-tuple-element.115, s32[]{:T(128)} %get-tuple-element.106), kind=kOutput, calls=%fused_computation.1.clone.1 | convolution fusion | flops 336855040 | bytes 2753024 | tf_op jit(solution)/shard_map/while/body/eval_jaxpr/sic,sje->ijce/dot_general | solution.py:23
  106.0 1.4 %copy.26 = bf16[8,80,32,32]{1,0,3,2:T(8,128)(2,1)S(1)} copy(bf16[8,80,32,32]{1,2,3,0:T(8,128)(2,1)S(1)} %fusion.18) | data formatting | bytes 2621440 | tf_op jit(solution)/shard_map/while/body/eval_jaxpr/convert_element_type | solution.py:26
  107.4 1.7 %reshape.22 = bf16[640,1024]{0,1:T(8,128)(2,1)S(1)} reshape(bf16[8,80,32,32]{1,0,3,2:T(8,128)(2,1)S(1)} %copy.26) | data formatting | bytes 2621440 | tf_op jit(solution)/shard_map/while/body/eval_jaxpr/reshape | solution.py:26
  109.1 1.6 %fusion.19 = bf16[640,128]{1,0:T(8,128)(2,1)S(1)} fusion(bf16[640,1024]{0,1:T(8,128)(2,1)S(1)} %reshape.22, bf16[1024,128]{1,0:T(8,128)(2,1)} %get-tuple-element.117, f32[128]{0:T(128)S(1)} %get-tuple-element.118), kind=kOutput, calls=%fused_computation.4.clone.1 | convolution fusion | flops 167936000 | bytes 1737216 | tf_op jit(solution)/shard_map/while/body/eval_jaxpr/dot_general | solution.py:27
  111.4 1.1 copy-done
  112.5 1.6 %fusion.18 = bf16[8,80,32,32]{1,2,3,0:T(8,128)(2,1)S(1)} fusion(bf16[256,80,32]{0,1,2:T(8,128)(2,1)S(1)} %get-tuple-element.116, bf16[4,256,8,32]{1,3,2,0:T(8,128)(2,1)} %get-tuple-element.115, s32[]{:T(128)} %get-tuple-element.106), kind=kOutput, calls=%fused_computation.1.clone.1 | convolution fusion | flops 336855040 | bytes 2753024 | tf_op jit(solution)/shard_map/while/body/eval_jaxpr/sic,sje->ijce/dot_general | solution.py:23
  114.1 1.4 %copy.26 = bf16[8,80,32,32]{1,0,3,2:T(8,128)(2,1)S(1)} copy(bf16[8,80,32,32]{1,2,3,0:T(8,128)(2,1)S(1)} %fusion.18) | data formatting | bytes 2621440 | tf_op jit(solution)/shard_map/while/body/eval_jaxpr/convert_element_type | solution.py:26
  115.5 1.7 %reshape.22 = bf16[640,1024]{0,1:T(8,128)(2,1)S(1)} reshape(bf16[8,80,32,32]{1,0,3,2:T(8,128)(2,1)S(1)} %copy.26) | data formatting | bytes 2621440 | tf_op jit(solution)/shard_map/while/body/eval_jaxpr/reshape | solution.py:26
  117.2 1.6 %fusion.19 = bf16[640,128]{1,0:T(8,128)(2,1)S(1)} fusion(bf16[640,1024]{0,1:T(8,128)(2,1)S(1)} %reshape.22, bf16[1024,128]{1,0:T(8,128)(2,1)} %get-tuple-element.117, f32[128]{0:T(128)S(1)} %get-tuple-element.118), kind=kOutput, calls=%fused_computation.4.clone.1 | convolution fusion | flops 167936000 | bytes 1737216 | tf_op jit(solution)/shard_map/while/body/eval_jaxpr/dot_general | solution.py:27
  (35 shorter events, 8.3 us)
Async XLA Ops:
  1.7 22.6 %all-to-all-start = ((bf16[16,2,512]{2,1,0:T(2,128)(2,1)}), bf16[16,2,512]{2,1,0:T(2,128)(2,1)S(1)}, u32[]{:S(2)}, u32[]{:S(2)}) async-start(bf16[16,2,512]{2,1,0:T(2,128)(2,1)} %reshape.17), calls=%async_computation | async-start | bytes 65536 | tf_op jit(solution)/shard_map/all_to_all | solution.py:40
  24.4 50.3 %all-to-all-start.1 = ((bf16[16,2,20480]{2,1,0:T(2,128)(2,1)}), bf16[16,2,20480]{2,1,0:T(2,128)(2,1)S(1)}, u32[]{:S(2)}, u32[]{:S(2)}) async-start(bf16[16,2,20480]{2,1,0:T(2,128)(2,1)} %reshape.19), calls=%async_computation.1 | async-start | bytes 2621440 | tf_op jit(solution)/shard_map/all_to_all | solution.py:41
  30.5 1.5 %collective-permute-start = (bf16[256,2,32]{2,0,1:T(8,128)(2,1)S(1)}, bf16[256,2,32]{2,0,1:T(8,128)(2,1)S(1)}, u32[]{:S(2)}, u32[]{:S(2)}) collective-permute-start(bf16[256,2,32]{2,0,1:T(8,128)(2,1)S(1)} %bitcast.53), channel_id=1, source_target_pairs={{0,1},{1,0},{2,3},{3,2},{4,5},{5,4},{6,7},{7,6},{8,9},{9,8},{10,11... | collective-permute-start | bytes 98312 | tf_op jit(solution)/shard_map/ppermute | solution.py:11
  32.1 10.7 %collective-permute-start.1 = (bf16[256,4,32]{0,2,1:T(8,128)(2,1)S(1)}, bf16[256,4,32]{0,2,1:T(8,128)(2,1)S(1)}, u32[]{:S(2)}, u32[]{:S(2)}) collective-permute-start(bf16[256,4,32]{0,2,1:T(8,128)(2,1)S(1)} %maximum_select_fusion.3), channel_id=1, source_target_pairs={{0,2},{1,3},{2,0},{3,1},{4,6},{5,7},{6,4},{7,5},{8,10},{9,11},{10,... | collective-permute-start | bytes 196616 | tf_op jit(solution)/shard_map/ppermute | solution.py:11
  42.8 12.6 %collective-permute-start.2 = (bf16[256,8,32]{0,2,1:T(8,128)(2,1)S(1)}, bf16[256,8,32]{0,2,1:T(8,128)(2,1)S(1)}, u32[]{:S(2)}, u32[]{:S(2)}) collective-permute-start(bf16[256,8,32]{0,2,1:T(8,128)(2,1)S(1)} %maximum_select_fusion.2), channel_id=1, source_target_pairs={{0,4},{1,5},{2,6},{3,7},{4,0},{5,1},{6,2},{7,3},{8,12},{9,13},{10,... | collective-permute-start | bytes 393224 | tf_op jit(solution)/shard_map/ppermute | solution.py:11
  55.5 18.3 %collective-permute-start.3 = (bf16[256,16,32]{0,2,1:T(8,128)(2,1)S(1)}, bf16[256,16,32]{0,2,1:T(8,128)(2,1)S(1)}, u32[]{:S(2)}, u32[]{:S(2)}) collective-permute-start(bf16[256,16,32]{0,2,1:T(8,128)(2,1)S(1)} %maximum_select_fusion.1), channel_id=1, source_target_pairs={{0,8},{1,9},{2,10},{3,11},{4,12},{5,13},{6,14},{7,15},{8,0},{9,1},... | collective-permute-start | bytes 786440 | tf_op jit(solution)/shard_map/ppermute | solution.py:11
  85.5 1.6 %copy-start.2 = (f32[128]{0:T(128)S(1)}, f32[128]{0:T(128)}, u32[]{:S(2)}) copy-start(f32[128]{0:T(128)} %param.9) | copy-start | bytes 1540
  87.1 1.1 copy-start
  92.9 2.3 %copy-start.1 = (bf16[256,80,32]{0,1,2:T(8,128)(2,1)S(1)}, bf16[256,80,32]{0,1,2:T(8,128)(2,1)}, u32[]{:S(2)}) copy-start(bf16[256,80,32]{0,1,2:T(8,128)(2,1)} %copy-done) | copy-start | bytes 3932164 | tf_op jit(solution)/shard_map/while
  95.2 1.1 copy-start
  101.0 2.3 %copy-start.1 = (bf16[256,80,32]{0,1,2:T(8,128)(2,1)S(1)}, bf16[256,80,32]{0,1,2:T(8,128)(2,1)}, u32[]{:S(2)}) copy-start(bf16[256,80,32]{0,1,2:T(8,128)(2,1)} %copy-done) | copy-start | bytes 3932164 | tf_op jit(solution)/shard_map/while
  103.3 1.1 copy-start
  109.1 2.3 %copy-start.1 = (bf16[256,80,32]{0,1,2:T(8,128)(2,1)S(1)}, bf16[256,80,32]{0,1,2:T(8,128)(2,1)}, u32[]{:S(2)}) copy-start(bf16[256,80,32]{0,1,2:T(8,128)(2,1)} %copy-done) | copy-start | bytes 3932164 | tf_op jit(solution)/shard_map/while
  111.4 1.1 copy-start
  117.2 2.3 %copy-start.1 = (bf16[256,80,32]{0,1,2:T(8,128)(2,1)S(1)}, bf16[256,80,32]{0,1,2:T(8,128)(2,1)}, u32[]{:S(2)}) copy-start(bf16[256,80,32]{0,1,2:T(8,128)(2,1)} %copy-done) | copy-start | bytes 3932164 | tf_op jit(solution)/shard_map/while
